TPU v7x, 32 devices: a whole 2x2x4 slice. The times are simulated.
32 devices in a mesh: dp: 4 (over z), row: 2 (over x), col: 4 (over y, core).
Axes of the slice: x: 2, y: 2, z: 4, core: 2. Of those that a mesh axis runs over, the one named last changes fastest.
Arguments:
- block_input: bfloat16 [8192, 1536], P('dp', 'row'), may hold values from -16 to 16
- positions: int32 [8192], P('dp'), may hold values from 0 to 511, as said below
- attn_gain: float32 [1536], P('row'), may hold values from 0.5 to 1.5
- w_qkv: bfloat16 [1536, 3072], P('row', 'col'), may hold values from -1.04613624 to 1.04613624
- w_out: bfloat16 [1536, 1536], P('col', 'row'), may hold values from -1.25 to 1.25
- ffn_gain: float32 [1536], P('row'), may hold values from 0.5 to 1.5
- w_gate: bfloat16 [1536, 4096], P('row', 'col'), may hold values from -0.15625 to 0.15625
- w_up: bfloat16 [1536, 4096], P('row', 'col'), may hold values from -0.15625 to 0.15625
- w_down: bfloat16 [4096, 1536], P('col', 'row'), may hold values from -0.09375 to 0.09375
- out_grad: bfloat16 [8192, 1536], P('dp', 'row'), may hold values from -6 to 6
Outputs:
- block_output: bfloat16 [8192, 1536], P('dp', 'row')
- input_grad: bfloat16 [8192, 1536], P('dp', 'row')
- attn_gain_grad: float32 [1536], P('row')
- w_qkv_grad: float32 [1536, 3072], P('row', 'col')
- w_out_grad: float32 [1536, 1536], P('col', 'row')
- ffn_gain_grad: float32 [1536], P('row')
- w_gate_grad: float32 [1536, 4096], P('row', 'col')
- w_up_grad: float32 [1536, 4096], P('row', 'col')
- w_down_grad: float32 [4096, 1536], P('col', 'row')
Inputs may be any that keep to these rules, and one draw needn't show every extreme that they name: `positions`: each sequence of 512 tokens holds one to five packed documents; a token's position counts from the first token of its document; some sequence is a single document.
All inputs are finite; a program needn't handle non-finite values.
Results may differ from a plain program's by a relative error of at most 0.015.
Values may be sent and summed in bfloat16 or wider, within the bound.
A program may use at most 192 MiB of HBM per device.

v0:
```python
import jax
import jax.numpy as jnp
from jax import lax
from jax.sharding import PartitionSpec as P

D = 1536
H = 16
KV = 8
HD = 96
SEQ_LEN = 512


EPS = 1e-05
THETA = 100000.0


def rotate(values, cosine, sine, sign):
    half = values.shape[-1] // 2
    first = values[..., :half]
    second = values[..., half:]
    return jnp.concatenate(
        [first * cosine - sign * second * sine, second * cosine + sign * first * sine], axis=-1
    )


def angle_tables(pos):
    freqs = THETA ** (-(jnp.arange(0, HD, 2).astype(jnp.float32) / HD))
    angles = pos.astype(jnp.float32)[..., None] * freqs
    return (jnp.cos(angles), jnp.sin(angles))


def norm_stat(values):
    return lax.psum(values, "row")


def width_total(values):
    return lax.psum(values, "col")


def join_rows(values):
    return lax.all_gather(values, "row", axis=0, tiled=True)


def split_rows(left, right, contract):
    return lax.psum_scatter(
        lax.dot_general(
            left, right, (((1,), (contract,)), ((), ())), preferred_element_type=jnp.float32
        ),
        "row",
        scatter_dimension=0,
        tiled=True,
    )


def left_product(left, right):
    return lax.dot_general(
        left, right, (((0,), (0,)), ((), ())), preferred_element_type=jnp.float32
    )


def right_product(left, right):
    return lax.dot_general(
        left, right, (((1,), (1,)), ((), ())), preferred_element_type=jnp.float32
    )


def swiglu_back(gate, up, grad):
    sig = jax.nn.sigmoid(gate)
    gate_grad = (grad * up * sig * (1.0 + gate * (1.0 - sig))).astype(jnp.bfloat16)
    up_grad = (grad * gate * sig).astype(jnp.bfloat16)
    return (gate_grad, up_grad)


def body(block_input, positions, attn_gain, w_qkv, w_out, ffn_gain, w_gate, w_up, w_down, out_grad):
    f32 = jnp.float32
    bf = jnp.bfloat16
    rows_all = block_input.shape[0]
    rows_half = rows_all // lax.axis_size("row")
    group = H // KV
    kv_local = w_qkv.shape[1] // ((group + 2) * HD)
    seqs_local = rows_half // SEQ_LEN
    scale = HD ** (-0.5)
    xf = block_input.astype(f32)
    inv1 = lax.rsqrt(norm_stat(jnp.sum(xf * xf, axis=1, keepdims=True)) / D + EPS)
    normed1 = (xf * inv1 * attn_gain).astype(bf)
    qkv_half = split_rows(normed1, w_qkv, 0)
    grouped = qkv_half.reshape(seqs_local, SEQ_LEN, kv_local, group + 2, HD)
    pos_half = lax.dynamic_slice_in_dim(
        positions, lax.axis_index("row") * rows_half, rows_half
    ).reshape(seqs_local, SEQ_LEN)
    cosine, sine = angle_tables(pos_half)
    cq = cosine[:, :, None, None, :]
    sq = sine[:, :, None, None, :]
    ck = cosine[:, :, None, :]
    sk = sine[:, :, None, :]
    queries = rotate(grouped[:, :, :, :group], cq, sq, 1.0).astype(bf)
    keys = rotate(grouped[:, :, :, group], ck, sk, 1.0).astype(bf)
    vals = grouped[:, :, :, group + 1].astype(bf)
    causal = jnp.arange(SEQ_LEN)[:, None] >= jnp.arange(SEQ_LEN)[None, :]
    scores = jnp.einsum("sikph,sjkh->skpij", queries, keys, preferred_element_type=f32) * scale
    scores = jnp.where(causal, scores, -1e30)
    top = jnp.max(scores, axis=-1, keepdims=True)
    lse = top + jnp.log(jnp.sum(jnp.exp(scores - top), axis=-1, keepdims=True))
    probs_b = jnp.exp(scores - lse).astype(bf)
    mixed = jnp.einsum("skpij,sjkh->sikph", probs_b, vals, preferred_element_type=f32).astype(bf)
    attn_rows = join_rows(mixed.reshape(rows_half, kv_local * group * HD))
    hidden = xf + width_total(jnp.dot(attn_rows, w_out, preferred_element_type=f32))
    inv2 = lax.rsqrt(norm_stat(jnp.sum(hidden * hidden, axis=1, keepdims=True)) / D + EPS)
    normed2 = (hidden * inv2 * ffn_gain).astype(bf)
    gate_part = jnp.dot(normed2, w_gate, preferred_element_type=f32)
    up_part = jnp.dot(normed2, w_up, preferred_element_type=f32)
    gate_kept, up_kept = (
        lax.psum_scatter(gate_part, "row", scatter_dimension=0, tiled=True),
        lax.psum_scatter(up_part, "row", scatter_dimension=0, tiled=True),
    )
    act_half = (jax.nn.silu(gate_kept) * up_kept).astype(bf)
    act_rows = lax.all_gather(act_half, "row", axis=0, tiled=True)
    block_output = (
        hidden + width_total(jnp.dot(act_rows, w_down, preferred_element_type=f32))
    ).astype(bf)
    w_down_grad = left_product(act_rows, out_grad)
    act_grad_part = right_product(out_grad, w_down)
    act_grad_half = lax.psum_scatter(act_grad_part, "row", scatter_dimension=0, tiled=True)
    gate_half, up_half = swiglu_back(gate_kept, up_kept, act_grad_half)
    gate_grad, up_grad = (
        lax.all_gather(gate_half, "row", axis=0, tiled=True),
        lax.all_gather(up_half, "row", axis=0, tiled=True),
    )
    w_gate_grad = left_product(normed2, gate_grad)
    w_up_grad = left_product(normed2, up_grad)
    normed2_grad = width_total(right_product(gate_grad, w_gate) + right_product(up_grad, w_up))
    ffn_gain_grad = jnp.sum(normed2_grad * hidden * inv2, axis=0)
    scaled2 = normed2_grad * ffn_gain
    hidden_grad = out_grad.astype(f32) + inv2 * (
        scaled2
        - hidden * inv2 * inv2 * norm_stat(jnp.sum(scaled2 * hidden, axis=1, keepdims=True)) / D
    )
    hidden_b = hidden_grad.astype(bf)
    w_out_grad = left_product(attn_rows, hidden_b)
    mixed_grad = (
        split_rows(hidden_b, w_out, 1).astype(bf).reshape(seqs_local, SEQ_LEN, kv_local, group, HD)
    )
    probs = jnp.exp(scores - lse)
    value_grad = jnp.einsum("skpij,sikph->sjkh", probs_b, mixed_grad, preferred_element_type=f32)
    prob_grad = jnp.einsum("sikph,sjkh->skpij", mixed_grad, vals, preferred_element_type=f32)
    delta = jnp.sum(mixed_grad.astype(f32) * mixed.astype(f32), axis=-1)
    delta = jnp.transpose(delta, (0, 2, 3, 1))[..., None]
    score_grad = (probs * (prob_grad - delta)).astype(bf)
    query_grad = rotate(
        jnp.einsum("skpij,sjkh->sikph", score_grad, keys, preferred_element_type=f32) * scale,
        cq,
        sq,
        -1.0,
    )
    key_grad = rotate(
        jnp.einsum("skpij,sikph->sjkh", score_grad, queries, preferred_element_type=f32) * scale,
        ck,
        sk,
        -1.0,
    )
    packed = jnp.concatenate(
        [query_grad, key_grad[:, :, :, None], value_grad[:, :, :, None]], axis=3
    ).astype(bf)
    qkv_grad = join_rows(packed.reshape(rows_half, w_qkv.shape[1]))
    w_qkv_grad = left_product(normed1, qkv_grad)
    normed1_grad = width_total(right_product(qkv_grad, w_qkv))
    attn_gain_grad = jnp.sum(normed1_grad * xf * inv1, axis=0)
    scaled1 = normed1_grad * attn_gain
    input_grad = (
        hidden_grad
        + inv1
        * (scaled1 - xf * inv1 * inv1 * norm_stat(jnp.sum(scaled1 * xf, axis=1, keepdims=True)) / D)
    ).astype(bf)
    attn_gain_grad, w_qkv_grad, w_out_grad, ffn_gain_grad, w_gate_grad, w_up_grad, w_down_grad = (
        lax.psum(attn_gain_grad.astype(jnp.bfloat16), "dp").astype(jnp.float32),
        lax.psum(w_qkv_grad.astype(jnp.bfloat16), "dp").astype(jnp.float32),
        lax.psum(w_out_grad.astype(jnp.bfloat16), "dp").astype(jnp.float32),
        lax.psum(ffn_gain_grad.astype(jnp.bfloat16), "dp").astype(jnp.float32),
        lax.psum(w_gate_grad.astype(jnp.bfloat16), "dp").astype(jnp.float32),
        lax.psum(w_up_grad.astype(jnp.bfloat16), "dp").astype(jnp.float32),
        lax.psum(w_down_grad.astype(jnp.bfloat16), "dp").astype(jnp.float32),
    )
    return (
        block_output,
        input_grad,
        attn_gain_grad,
        w_qkv_grad,
        w_out_grad,
        ffn_gain_grad,
        w_gate_grad,
        w_up_grad,
        w_down_grad,
    )


def solution(mesh):
    return jax.shard_map(
        body,
        mesh=mesh,
        in_specs=(
            P("dp", "row"),
            P("dp"),
            P("row"),
            P("row", "col"),
            P("col", "row"),
            P("row"),
            P("row", "col"),
            P("row", "col"),
            P("col", "row"),
            P("dp", "row"),
        ),
        out_specs=(
            P("dp", "row"),
            P("dp", "row"),
            P("row"),
            P("row", "col"),
            P("col", "row"),
            P("row"),
            P("row", "col"),
            P("row", "col"),
            P("col", "row"),
        ),
        check_vma=False,
    )
```

profile of v0, /device:TPU:0, one launch (start us, length us, event | category | flops | bytes accessed | tf_op | source)
XLA Modules:
  0.0 1491.3 jit_solution(6194909048291860447)
XLA Ops:
  9.9 5.9 psum.105
  15.9 7.6 fusion.30
  25.0 77.5 %reduce-scatter.6.cloned.1.call-done = f32[1024,768]{1,0:T(8,128)} async-done(((f32[2048,768]{1,0:T(8,128)}), f32[1024,768]{1,0:T(8,128)}) %reduce-scatter.6.cloned.1.call-update) | async-done | bytes 3145744 | tf_op jit(solution)/shard_map/reduce_scatter | solution.py:45
  106.1 5.6 reshape.64
  126.9 27.1 %all-gather.6.cloned.1.call-done = bf16[2048,384]{0,1:T(8,128)(2,1)} async-done(((bf16[1024,384]{0,1:T(8,128)(2,1)}), bf16[2048,384]{0,1:T(8,128)(2,1)}) %all-gather.6.cloned.1.call-update) | async-done | bytes 1572880 | tf_op jit(solution)/shard_map/all_gather | solution.py:41
  154.0 6.0 fusion.42
  160.1 9.1 fusion.46
  169.3 110.5 %all-reduce.8.cloned.1.call-done = f32[2048,768]{1,0:T(8,128)} async-done(((f32[2048,768]{1,0:T(8,128)}), f32[2048,768]{1,0:T(8,128)}) %all-reduce.8.cloned.1.call-update) | async-done | bytes 6291472 | tf_op jit(solution)/shard_map/psum | solution.py:37
  279.8 7.2 multiply_reduce_fusion.2
  297.4 5.6 fusion.44
  303.1 7.6 fusion.43
  310.8 70.9 %reduce-scatter.12.cloned.1.call-done = f32[1024,1024]{1,0:T(8,128)} async-done(((f32[2048,1024]{1,0:T(8,128)}), f32[1024,1024]{1,0:T(8,128)}) %reduce-scatter.12.cloned.1.call-update) | async-done | bytes 4194320 | tf_op jit(solution)/shard_map/reduce_scatter | solution.py:123
  381.7 101.5 %reduce-scatter.10.cloned.1.call-done = f32[1024,1024]{1,0:T(8,128)} async-done(((f32[2048,1024]{1,0:T(8,128)}), f32[1024,1024]{1,0:T(8,128)}) %reduce-scatter.10.cloned.1.call-update) | async-done | bytes 4194320 | tf_op jit(solution)/shard_map/reduce_scatter | solution.py:114
  483.2 101.5 %reduce-scatter.8.cloned.1.call-done = f32[1024,1024]{1,0:T(8,128)} async-done(((f32[2048,1024]{1,0:T(8,128)}), f32[1024,1024]{1,0:T(8,128)}) %reduce-scatter.8.cloned.1.call-update) | async-done | bytes 4194320 | tf_op jit(solution)/shard_map/reduce_scatter | solution.py:113
  584.7 8.1 multiply_convert_fusion.1
  594.1 55.6 %all-gather.10.cloned.1.call-done = bf16[2048,1024]{1,0:T(8,128)(2,1)} async-done(((bf16[1024,1024]{1,0:T(8,128)(2,1)}), bf16[2048,1024]{1,0:T(8,128)(2,1)}) %all-gather.10.cloned.1.call-update) | async-done | bytes 4194320 | tf_op jit(solution)/shard_map/all_gather | solution.py:126
  649.7 8.3 fusion.47
  658.0 50.6 %all-gather.12.cloned.1.call-done = bf16[2048,1024]{1,0:T(8,128)(2,1)} async-done(((bf16[1024,1024]{1,0:T(8,128)(2,1)}), bf16[2048,1024]{1,0:T(8,128)(2,1)}) %all-gather.12.cloned.1.call-update) | async-done | bytes 4194320 | tf_op jit(solution)/shard_map/all_gather | solution.py:127
  708.6 10.6 convolution_add_fusion
  719.3 119.7 %all-reduce.10.cloned.1.call-done = f32[2048,768]{1,0:T(8,128)} async-done(((f32[2048,768]{1,0:T(8,128)}), f32[2048,768]{1,0:T(8,128)}) %all-reduce.10.cloned.1.call-update) | async-done | bytes 6291472 | tf_op jit(solution)/shard_map/psum | solution.py:37
  839.0 5.4 multiply_reduce_fusion
  849.4 6.7 multiply_add_fusion
  863.2 42.8 %reduce-scatter.14.cloned.1.call-done = f32[1024,384]{1,0:T(8,128)} async-done(((f32[2048,384]{1,0:T(8,128)}), f32[1024,384]{1,0:T(8,128)}) %reduce-scatter.14.cloned.1.call-update) | async-done | bytes 1572880 | tf_op jit(solution)/shard_map/reduce_scatter | solution.py:45
  925.8 39.1 %all-gather.8.cloned.1.call-done = bf16[2048,1024]{1,0:T(8,128)(2,1)} async-done(((bf16[1024,1024]{1,0:T(8,128)(2,1)}), bf16[2048,1024]{1,0:T(8,128)(2,1)}) %all-gather.8.cloned.1.call-update) | async-done | bytes 4194320 | tf_op jit(solution)/shard_map/all_gather | solution.py:117
  964.9 8.2 fusion.45
  973.1 38.7 %all-gather.14.cloned.1.call-done = bf16[2048,768]{0,1:T(8,128)(2,1)} async-done(((bf16[1024,768]{0,1:T(8,128)(2,1)}), bf16[2048,768]{0,1:T(8,128)(2,1)}) %all-gather.14.cloned.1.call-update) | async-done | bytes 3145744 | tf_op jit(solution)/shard_map/all_gather | solution.py:41
  1011.8 7.2 fusion.48
  1019.4 8.0 convolution_convert_fusion
  1043.9 196.1 %all-reduce.12.cloned.1.call-done = (f32[2048,768]{1,0:T(8,128)}, f32[2048,768]{1,0:T(8,128)}) async-done(((f32[2048,768]{1,0:T(8,128)}, f32[2048,768]{1,0:T(8,128)}), (f32[2048,768]{1,0:T(8,128)}, f32[2048,768]{1,0:T(8,128)})) %all-reduce.12.cloned.1.call-update) | async-done | bytes 12582928 | tf_op jit(solution)/shard_map/psum | solution.py:37
  1244.8 12.2 all-reduce.1
  1263.4 7.1 add_convert_fusion
  1277.0 196.2 %all-reduce.14.cloned.1.call-done = (bf16[768,768]{1,0:T(8,128)(2,1)}, bf16[384,768]{1,0:T(8,128)(2,1)}, bf16[768,1024]{1,0:T(8,128)(2,1)}, bf16[768,1024]{1,0:T(8,128)(2,1)}, bf16[1024,768]{1,0:T(8,128)(2,1)}) async-done(((bf16[768,768]{1,0:T(8,128)(2,1)}, bf16[384,768]{1,0:T(8,128)(2,1)}, bf16[768,1024]{1,0:T(8,128)(2,1)}, bf16[768,1024]{1,0:T(8,128)(2,1)}, bf16[1024,768]{1,0:T(8,128)(2,1)}), ...) | async-done | bytes 6488080 | tf_op jit(solution)/shard_map/psum | solution.py:176
  (169 shorter events, 112.3 us)
Async XLA Ops:
  7.2 295.9 %copy-start = (bf16[768,1024]{1,0:T(8,128)(2,1)S(1)}, bf16[768,1024]{1,0:T(8,128)(2,1)}, u32[]{:S(2)}) copy-start(bf16[768,1024]{1,0:T(8,128)(2,1)} %param.16) | copy-start | bytes 4718596
  7.2 95.4 %reduce-scatter.6.cloned.1.call-start = ((), (), s32[]{:S(2)}) async-start(), calls=%async_computation.5 | async-start | bytes 9437184 | tf_op jit(solution)/shard_map/reduce_scatter | solution.py:45
  23.5 130.5 %all-gather.6.cloned.1.call-start = ((), (), s32[]{:S(2)}) async-start(), calls=%async_computation.6 | async-start | bytes 2359296 | tf_op jit(solution)/shard_map/all_gather | solution.py:41
  24.3 93.4 %copy-start.18 = (pred[512,512]{0,1:T(8,128)(4,1)}, pred[512,512]{0,1:T(8,128)(4,1)S(1)}, u32[]{:S(2)}) copy-start(pred[512,512]{0,1:T(8,128)(4,1)S(1)} %iota_compare_fusion) | copy-start | bytes 786436
  113.2 6.3 copy-start.24
  126.7 153.1 %all-reduce.8.cloned.1.call-start = ((), (), s32[]{:S(2)}) async-start(), calls=%async_computation.7 | async-start | bytes 12582912 | tf_op jit(solution)/shard_map/psum | solution.py:37
  160.1 221.6 %reduce-scatter.12.cloned.1.call-start = ((), (), s32[]{:S(2)}) async-start(), calls=%async_computation.11 | async-start | bytes 12582912 | tf_op jit(solution)/shard_map/reduce_scatter | solution.py:123
  169.3 122.9 %copy-start.25 = (f32[768]{0:T(1024)S(1)}, f32[768]{0:T(1024)}, u32[]{:S(2)}) copy-start(f32[768]{0:T(1024)} %param.15) | copy-start | bytes 9220
  169.3 313.9 %reduce-scatter.10.cloned.1.call-start = ((), (), s32[]{:S(2)}) async-start(), calls=%async_computation.9 | async-start | bytes 12582912 | tf_op jit(solution)/shard_map/reduce_scatter | solution.py:114
  292.2 5.2 copy-start.33
  303.0 281.6 %reduce-scatter.8.cloned.1.call-start = ((), (), s32[]{:S(2)}) async-start(), calls=%async_computation.8 | async-start | bytes 12582912 | tf_op jit(solution)/shard_map/reduce_scatter | solution.py:113
  310.7 339.0 %all-gather.10.cloned.1.call-start = ((), (), s32[]{:S(2)}) async-start(), calls=%async_computation.12 | async-start | bytes 6291456 | tf_op jit(solution)/shard_map/all_gather | solution.py:126
  592.8 115.8 %all-gather.12.cloned.1.call-start = ((), (), s32[]{:S(2)}) async-start(), calls=%async_computation.13 | async-start | bytes 6291456 | tf_op jit(solution)/shard_map/all_gather | solution.py:127
  593.6 245.4 %all-reduce.10.cloned.1.call-start = ((), (), s32[]{:S(2)}) async-start(), calls=%async_computation.14 | async-start | bytes 12582912 | tf_op jit(solution)/shard_map/psum | solution.py:37
  719.2 186.8 %reduce-scatter.14.cloned.1.call-start = ((), (), s32[]{:S(2)}) async-start(), calls=%async_computation.15 | async-start | bytes 4718592 | tf_op jit(solution)/shard_map/reduce_scatter | solution.py:45
  849.4 9.3 copy-start.10
  862.2 102.7 %all-gather.8.cloned.1.call-start = ((), (), s32[]{:S(2)}) async-start(), calls=%async_computation.10 | async-start | bytes 6291456 | tf_op jit(solution)/shard_map/all_gather | solution.py:117
  863.0 148.8 %all-gather.14.cloned.1.call-start = ((), (), s32[]{:S(2)}) async-start(), calls=%async_computation.16 | async-start | bytes 4718592 | tf_op jit(solution)/shard_map/all_gather | solution.py:41
  909.8 5.4 copy-start.15
  909.8 5.4 copy-start.17
  922.5 42.4 %copy-start.34 = (bf16[1024,768]{1,0:T(8,128)(2,1)S(1)}, bf16[1024,768]{1,0:T(8,128)(2,1)}, u32[]{:S(2)}) copy-start(bf16[1024,768]{1,0:T(8,128)(2,1)} %param.18) | copy-start | bytes 4718596
  925.8 86.1 %copy-start.35 = (bf16[768,768]{1,0:T(8,128)(2,1)S(1)}, bf16[768,768]{1,0:T(8,128)(2,1)}, u32[]{:S(2)}) copy-start(bf16[768,768]{1,0:T(8,128)(2,1)} %param.13) | copy-start | bytes 3538948
  925.8 314.2 %all-reduce.12.cloned.1.call-start = ((), (), s32[]{:S(2)}) async-start(), calls=%async_computation.17 | async-start | bytes 25165824 | tf_op jit(solution)/shard_map/psum | solution.py:37
  1019.1 454.2 %all-reduce.14.cloned.1.call-start = ((), (), s32[]{:S(2)}) async-start(), calls=%async_computation.18 | async-start | bytes 12976128 | tf_op jit(solution)/shard_map/psum | solution.py:176
  1019.3 8.0 copy-start.8
  1019.4 8.0 copy-start.30
  1027.3 9.1 slice-start
  1263.4 7.1 slice-start.2
  1263.4 7.1 slice-start.3
  1263.4 8.5 copy-start.4
  1263.4 10.4 copy-start.5
  1473.3 7.2 copy-start.12
  (25 other events, 70.2 us)
Sparse Core Ops, SparseCore 0:
  23.6 78.9 reduce-scatter.5
  126.8 27.1 all-gather.5
  160.2 119.5 all-reduce.7
  282.0 99.6 reduce-scatter.11
  383.8 99.3 reduce-scatter.9
  485.3 99.2 reduce-scatter.7
  593.0 56.7 all-gather.9
  651.9 56.7 all-gather.11
  719.4 119.5 all-reduce.9
  862.4 43.6 reduce-scatter.13
  908.1 56.7 all-gather.7
  966.9 44.8 all-gather.13
  1019.2 220.6 all-reduce.11
  1243.7 229.5 all-reduce.13
where the time goes:
time: 1490 us
  waiting for transfers between devices  1230 us (83%)
  matrix products  112 us (8%)
  other arithmetic  66.5 us (4%)
  blocking collectives  33.5 us (2%)
  local copies, waits for them, and re-layouts  33.1 us (2%)
    psum x3, waiting for transfers between devices, width_total(): return lax.psum(values, 'col')  426 us
    psum x1, waiting for transfers between devices, body(): lax.psum(w_qkv_grad.astype(jnp.bfloat16), 'dp').astype(jnp.float32)  196 us
    reduce_scatter x2, waiting for transfers between devices, split_rows(): lax.psum_scatter(lax.dot_general(left, right, (((1,), (contract,)), ((),...  120 us
    reduce_scatter x1, waiting for transfers between devices, body(): lax.psum_scatter(up_part, 'row', scatter_dimension=0, tiled=True)  102 us
    reduce_scatter x1, waiting for transfers between devices, body(): lax.psum_scatter(gate_part, 'row', scatter_dimension=0, tiled=True)  101 us
    reduce_scatter x1, waiting for transfers between devices, body(): lax.psum_scatter(act_grad_part, 'row', scatter_dimension=0, tiled=True)  70.9 us
    all_gather x2, waiting for transfers between devices, join_rows(): return lax.all_gather(values, 'row', axis=0, tiled=True)  65.8 us
    all_gather x1, waiting for transfers between devices, body(): lax.all_gather(gate_half, 'row', axis=0, tiled=True)  55.6 us
  transfers between devices with their start and end apart: 14, of which 14 were waited for; matrix products, arithmetic and copies ran while one was open for 7% of the time, Pallas kernels for 0%

commit v1 on v0

v1 whole, which is shorter than its diff:
```python
import jax
import jax.numpy as jnp
from jax import lax
from jax.experimental import pallas as pl
from jax.experimental.pallas import tpu as pltpu
from jax.sharding import PartitionSpec as P

HD = 96
GROUP = 2
SEQ_LEN = 512
EPS = 1e-05
THETA = 100000.0
MESH = pl.DeviceIdType.MESH
f32 = jnp.float32
bf = jnp.bfloat16


class Net:
    def __init__(self, send_sem, recv_sem, row=True, col=True):
        self.row, self.col = lax.axis_index("row"), lax.axis_index("col")
        self.core = lax.rem(self.col, 2)
        self.y = self.col // 2
        self.far = lax.rem(self.col + 2, 4)
        self.px = {"row": 1 - self.row}
        self.py = {"col": self.far}
        self.pc = {"col": 2 * self.y + 1 - self.core}
        self.send_sem, self.recv_sem, self.n = send_sem, recv_sem, 0
        self.copies = []
        barrier = pltpu.get_barrier_semaphore()
        partners = ([self.px] if row else []) + ([self.py, self.pc] if col else [])
        for partner in partners:
            pl.semaphore_signal(barrier, inc=1, device_id=partner, device_id_type=MESH)
        pl.semaphore_wait(barrier, len(partners))

    def send(self, src, dst, partner):
        copy = pltpu.make_async_remote_copy(
            src_ref=src,
            dst_ref=dst,
            send_sem=self.send_sem.at[self.n],
            recv_sem=self.recv_sem.at[self.n],
            device_id=partner,
            device_id_type=MESH,
        )
        self.n += 1
        copy.start()
        self.copies.append(copy)
        return copy

    def drain(self):
        for copy in self.copies:
            copy.wait_send()


def ds(start, size, unit):
    return pl.ds(pl.multiple_of(start, unit), size)


def comm_call(kernel, outs, scratch, copies, cid, *args, local=0, nbytes=0, any_in=False):
    vm = pl.BlockSpec(memory_space=pltpu.VMEM)
    sems = [pltpu.SemaphoreType.DMA((copies,)), pltpu.SemaphoreType.DMA((copies,))]
    if local:
        sems.append(pltpu.SemaphoreType.DMA((local,)))
    return pl.pallas_call(
        kernel,
        out_shape=outs,
        in_specs=[pl.BlockSpec(memory_space=pl.ANY) if any_in else vm] * len(args),
        out_specs=[vm] * len(outs),
        scratch_shapes=scratch + sems,
        compiler_params=pltpu.CompilerParams(
            collective_id=cid, has_side_effects=True, vmem_limit_bytes=56 * 2**20
        ),
        cost_estimate=pl.CostEstimate(flops=0, bytes_accessed=nbytes, transcendentals=0),
    )(*args)


def fetch_kernel(x_ref, dy_ref, xo, dyo, ssem, rsem, lsem):
    net = Net(ssem, rsem)
    rows, wide = x_ref.shape
    part = rows // 2
    block = part // 4
    own, peer = net.row * wide, (1 - net.row) * wide
    streams = [
        (x_ref, (1 - net.row) * part, xo, 0),
        (dy_ref, 0, dyo, 0),
        (dy_ref, part, dyo, part),
    ]
    first = [
        net.send(
            src.at[ds(sb + net.col * block, block, 16), :],
            out.at[ds(db + net.col * block, block, 16), ds(own, wide, 128)],
            net.px,
        )
        for src, sb, out, db in streams
    ]
    local = [
        pltpu.make_async_copy(
            x_ref.at[ds(net.row * part, part, 16), :], xo.at[:, ds(own, wide, 128)], lsem.at[0]
        ),
        pltpu.make_async_copy(dy_ref, dyo.at[:, ds(own, wide, 128)], lsem.at[1]),
    ]
    for copy in local:
        copy.start()

    def spot(stream, col):
        return stream[2].at[ds(stream[3] + col * block, block, 16), ds(peer, wide, 128)]

    over_y, over_c = [], []
    for stream, copy in zip(streams, first):
        copy.wait_recv()
        here = spot(stream, net.col)
        over_y.append(net.send(here, here, net.py))
        over_c.append(net.send(here, here, net.pc))
    for stream, copy in zip(streams, over_y):
        copy.wait_recv()
        there = spot(stream, net.far)
        over_c.append(net.send(there, there, net.pc))
    for copy in over_c:
        copy.wait_recv()
    for copy in local:
        copy.wait()
    net.drain()


def fetch(x, dy):
    rows, wide = x.shape
    return comm_call(
        fetch_kernel,
        [
            jax.ShapeDtypeStruct((rows // 2, 2 * wide), x.dtype),
            jax.ShapeDtypeStruct((rows, 2 * wide), dy.dtype),
        ],
        [],
        12,
        1,
        x,
        dy,
        local=2,
        nbytes=4 * x.size * 6,
        any_in=True,
    )


def spread_kernel(h_ref, out, ssem, rsem, lsem):
    net = Net(ssem, rsem)
    block, wide = h_ref.shape[0], h_ref.shape[1] // 2
    part = out.shape[0] // 2
    own, peer = net.row * wide, (1 - net.row) * wide

    def spot(row, col):
        return out.at[ds(row * part + col * block, block, 16), :]

    mine = spot(net.row, net.col)
    over_x = net.send(h_ref.at[:, ds(peer, wide, 128)], mine, net.px)
    half = h_ref.at[:, ds(own, wide, 128)]
    over_y = [net.send(half, mine, net.py)]
    over_c = [net.send(half, mine, net.pc)]
    local = pltpu.make_async_copy(half, mine, lsem.at[0])
    local.start()
    over_x.wait_recv()
    theirs = spot(1 - net.row, net.col)
    over_y.append(net.send(theirs, theirs, net.py))
    over_c.append(net.send(theirs, theirs, net.pc))
    for row, copy in zip((net.row, 1 - net.row), over_y):
        copy.wait_recv()
        there = spot(row, net.far)
        over_c.append(net.send(there, there, net.pc))
    for copy in over_c:
        copy.wait_recv()
    local.wait()
    net.drain()


def spread(h, rows):
    return comm_call(
        spread_kernel,
        [jax.ShapeDtypeStruct((rows, h.shape[1] // 2), h.dtype)],
        [],
        7,
        2,
        h,
        local=1,
        nbytes=rows * h.shape[1] * 8,
    )[0]


def gather_col_kernel(h_ref, out, ssem, rsem, lsem):
    net = Net(ssem, rsem, row=False)
    block = h_ref.shape[0]

    def spot(col):
        return out.at[ds(col * block, block, 16), :]

    mine = spot(net.col)
    over_y = net.send(h_ref, mine, net.py)
    over_c = [net.send(h_ref, mine, net.pc)]
    local = pltpu.make_async_copy(h_ref, mine, lsem.at[0])
    local.start()
    over_y.wait_recv()
    there = spot(net.far)
    over_c.append(net.send(there, there, net.pc))
    for copy in over_c:
        copy.wait_recv()
    local.wait()
    net.drain()


def gather_col(h):
    return comm_call(
        gather_col_kernel,
        [jax.ShapeDtypeStruct((4 * h.shape[0], h.shape[1]), h.dtype)],
        [],
        3,
        3,
        h,
        local=1,
        nbytes=h.size * 24,
    )[0]


def add_rows(dst, terms, rows):
    step = 32

    def one(i, carry):
        at = pl.multiple_of(i * step, step)
        total = None
        for ref, base in terms:
            piece = ref[pl.ds(pl.multiple_of(base + at, 16), step), :].astype(f32)
            total = piece if total is None else total + piece
        ref, base = dst
        ref[pl.ds(pl.multiple_of(base + at, 16), step), :] = total.astype(ref.dtype)
        return carry

    lax.fori_loop(0, rows // step, one, 0)


def reduce_col_kernel(p_ref, out, near, mid, far, ssem, rsem):
    net = Net(ssem, rsem, row=False)
    rows = p_ref.shape[0] // 4
    pieces = 2
    size = rows // pieces
    over_c = []
    for y in (1 - net.y, net.y):
        for i in range(pieces):
            n = len(over_c)
            base = (2 * y + 1 - net.core) * rows + i * size
            over_c.append(
                net.send(p_ref.at[ds(base, size, 16), :], near.at[pl.ds(n * size, size), :], net.pc)
            )
    over_y = []
    for i in range(pieces):
        over_c[i].wait_recv()
        base = net.far * rows + i * size
        add_rows((mid, i * size), [(p_ref, base), (near, i * size)], size)
        here = pl.ds(i * size, size)
        over_y.append(net.send(mid.at[here, :], far.at[here, :], net.py))
    for i in range(pieces):
        over_c[pieces + i].wait_recv()
    for i in range(pieces):
        over_y[i].wait_recv()
        base = net.col * rows + i * size
        add_rows(
            (out, i * size),
            [(p_ref, base), (near, rows + i * size), (far, i * size)],
            size,
        )
    net.drain()


def reduce_col(p):
    rows, wide = p.shape[0] // 4, p.shape[1]
    return comm_call(
        reduce_col_kernel,
        [jax.ShapeDtypeStruct((rows, wide), f32)],
        [
            pltpu.VMEM((2 * rows, wide), p.dtype),
            pltpu.VMEM((rows, wide), p.dtype),
            pltpu.VMEM((rows, wide), p.dtype),
        ],
        6,
        4,
        p,
        nbytes=p.size * 6,
    )[0]


def gather_all_kernel(h_ref, out, ssem, rsem, lsem):
    net = Net(ssem, rsem)
    block = h_ref.shape[0]
    half = block // 2

    def spot(row, col, part):
        return out.at[ds((row * 4 + col) * block + part * half, half, 16), :]

    a, b = h_ref.at[pl.ds(0, half), :], h_ref.at[pl.ds(half, half), :]
    mine_a, mine_b = spot(net.row, net.col, 0), spot(net.row, net.col, 1)
    y_a = net.send(a, mine_a, net.py)
    x_b = net.send(b, mine_b, net.px)
    x_a = net.send(a, mine_a, net.px)
    y_b = net.send(b, mine_b, net.py)
    over_c = [net.send(a, mine_a, net.pc), net.send(b, mine_b, net.pc)]
    local = pltpu.make_async_copy(
        h_ref, out.at[ds((net.row * 4 + net.col) * block, block, 16), :], lsem.at[0]
    )
    local.start()
    y_a.wait_recv()
    got = spot(net.row, net.far, 0)
    x_ya = net.send(got, got, net.px)
    over_c.append(net.send(got, got, net.pc))
    x_b.wait_recv()
    got = spot(1 - net.row, net.col, 1)
    y_xb = net.send(got, got, net.py)
    over_c.append(net.send(got, got, net.pc))
    for copy, row, col, part in (
        (x_a, 1 - net.row, net.col, 0),
        (y_b, net.row, net.far, 1),
        (x_ya, 1 - net.row, net.far, 0),
        (y_xb, 1 - net.row, net.far, 1),
    ):
        copy.wait_recv()
        got = spot(row, col, part)
        over_c.append(net.send(got, got, net.pc))
    for copy in over_c:
        copy.wait_recv()
    local.wait()
    net.drain()


def gather_all(h):
    return comm_call(
        gather_all_kernel,
        [jax.ShapeDtypeStruct((8 * h.shape[0], h.shape[1]), h.dtype)],
        [],
        14,
        5,
        h,
        local=1,
        nbytes=h.size * 40,
    )[0]


def reduce_all_kernel(p_ref, out, near, mid, far, ssem, rsem):
    net = Net(ssem, rsem)
    block = p_ref.shape[0] // 8
    half = block // 2
    nx, ny = 1 - net.row, 1 - net.y
    order = [
        (nx, ny, 0),
        (nx, ny, 1),
        (nx, net.y, 0),
        (net.row, ny, 1),
        (net.row, ny, 0),
        (nx, net.y, 1),
        (net.row, net.y, 0),
        (net.row, net.y, 1),
    ]

    def base(i, core):
        x, y, part = order[i]
        return (x * 4 + 2 * y + core) * block + part * half

    def at(i):
        return pl.ds(i * half, half)

    over_c = [
        net.send(p_ref.at[ds(base(i, 1 - net.core), half, 16), :], near.at[at(i), :], net.pc)
        for i in range(8)
    ]
    sent = []
    for i in range(6):
        over_c[i].wait_recv()
        terms = [(p_ref, base(i, net.core)), (near, i * half)]
        if i >= 4:
            sent[i - 4].wait_recv()
            terms.append((far, (i - 4) * half))
        add_rows((mid, i * half), terms, half)
        sent.append(
            net.send(mid.at[at(i), :], far.at[at(i), :], net.px if i in (0, 2, 5) else net.py)
        )
    for i in (6, 7):
        over_c[i].wait_recv()
        sent[i - 4].wait_recv()
        sent[i - 2].wait_recv()
        add_rows(
            (out, (i - 6) * half),
            [
                (p_ref, base(i, net.core)),
                (near, i * half),
                (far, (i - 4) * half),
                (far, (i - 2) * half),
            ],
            half,
        )
    net.drain()


def reduce_all(p):
    rows, wide = p.shape[0] // 8, p.shape[1]
    return comm_call(
        reduce_all_kernel,
        [jax.ShapeDtypeStruct((rows, wide), f32)],
        [
            pltpu.VMEM((4 * rows, wide), p.dtype),
            pltpu.VMEM((3 * rows, wide), p.dtype),
            pltpu.VMEM((3 * rows, wide), p.dtype),
        ],
        14,
        6,
        p,
        nbytes=p.size * 6,
    )[0]


def rotate(values, cosine, sine, sign):
    half = values.shape[-1] // 2
    first = values[..., :half]
    second = values[..., half:]
    return jnp.concatenate(
        [first * cosine - sign * second * sine, second * cosine + sign * first * sine], axis=-1
    )


def angle_tables(pos):
    freqs = THETA ** (-(jnp.arange(0, HD, 2).astype(jnp.float32) / HD))
    angles = pos.astype(jnp.float32)[..., None] * freqs
    return (jnp.cos(angles), jnp.sin(angles))


def dot(left, right, lhs, rhs, out=f32):
    return lax.dot_general(
        left, right, (((lhs,), (rhs,)), ((), ())), preferred_element_type=f32
    ).astype(out)


def swap(values):
    return lax.ppermute(values, "row", [(0, 1), (1, 0)])


def in_order(row, own, peer, axis):
    return jnp.where(
        row == 0,
        jnp.concatenate([own, peer], axis=axis),
        jnp.concatenate([peer, own], axis=axis),
    )


def half_of(values, index, axis):
    size = values.shape[axis] // 2
    return lax.dynamic_slice_in_dim(values, index * size, size, axis)


def body(block_input, positions, attn_gain, w_qkv, w_out, ffn_gain, w_gate, w_up, w_down, out_grad):
    row, col = lax.axis_index("row"), lax.axis_index("col")
    n_dp = lax.axis_size("dp")
    rows_all, half_wide = block_input.shape
    rows_half = rows_all // 2
    rows_own = rows_half // 4
    wide = 2 * half_wide
    kv_local = w_qkv.shape[1] // ((GROUP + 2) * HD)
    seqs = rows_half // SEQ_LEN
    scale = HD ** (-0.5)

    gains = jnp.stack([attn_gain, ffn_gain])
    gains_peer = swap(gains)
    wq_peer = swap(w_qkv)
    x_rows, dy_all = fetch(block_input, out_grad)
    w_out_l, w_gate_l, w_up_l, w_down_l, wq_peer = lax.optimization_barrier(
        (w_out, w_gate, w_up, w_down, wq_peer)
    )
    gains_all = in_order(row, gains, gains_peer, 1)
    g1, g2 = gains_all[0], gains_all[1]
    wq = in_order(row, w_qkv, wq_peer, 0)
    wo = in_order(row, w_out_l, swap(w_out_l), 1)
    gu = jnp.stack([w_gate_l, w_up_l], axis=1)
    units = gu.shape[2] // 2
    gu_mine = half_of(gu, row, 2).reshape(half_wide, 2 * units)
    gu_theirs = half_of(gu, 1 - row, 2).reshape(half_wide, 2 * units)
    wgu = in_order(row, gu_mine, swap(gu_theirs), 0)
    wd = in_order(row, half_of(w_down_l, row, 0), swap(half_of(w_down_l, 1 - row, 0)), 1)

    xf = x_rows.astype(f32)
    inv1 = lax.rsqrt(jnp.sum(xf * xf, axis=1, keepdims=True) / wide + EPS)
    normed1 = (xf * inv1 * g1).astype(bf)
    qkv = dot(normed1, wq, 1, 0)
    grouped = qkv.reshape(seqs, SEQ_LEN, kv_local, GROUP + 2, HD)
    pos = half_of(positions, row, 0).reshape(seqs, SEQ_LEN)
    cosine, sine = angle_tables(pos)
    cq = cosine[:, :, None, None, :]
    sq = sine[:, :, None, None, :]
    ck = cosine[:, :, None, :]
    sk = sine[:, :, None, :]
    queries = rotate(grouped[:, :, :, :GROUP], cq, sq, 1.0).astype(bf)
    keys = rotate(grouped[:, :, :, GROUP], ck, sk, 1.0).astype(bf)
    vals = grouped[:, :, :, GROUP + 1].astype(bf)
    causal = jnp.arange(SEQ_LEN)[:, None] >= jnp.arange(SEQ_LEN)[None, :]
    scores = jnp.einsum("sikph,sjkh->skpij", queries, keys, preferred_element_type=f32) * scale
    scores = jnp.where(causal, scores, -1e30)
    top = jnp.max(scores, axis=-1, keepdims=True)
    lse = top + jnp.log(jnp.sum(jnp.exp(scores - top), axis=-1, keepdims=True))
    probs_b = jnp.exp(scores - lse).astype(bf)
    mixed = jnp.einsum("skpij,sjkh->sikph", probs_b, vals, preferred_element_type=f32).astype(bf)
    attn_rows = mixed.reshape(rows_half, kv_local * GROUP * HD)

    x_own = lax.dynamic_slice_in_dim(x_rows, col * rows_own, rows_own, 0).astype(f32)
    inv1_own = lax.dynamic_slice_in_dim(inv1, col * rows_own, rows_own, 0)
    hidden = x_own + reduce_col(dot(attn_rows, wo, 1, 0, bf))
    inv2 = lax.rsqrt(jnp.sum(hidden * hidden, axis=1, keepdims=True) / wide + EPS)
    normed2 = gather_all((hidden * inv2 * g2).astype(bf))

    both = dot(normed2, wgu, 1, 0)
    gate, up = both[:, :units], both[:, units:]
    sig = jax.nn.sigmoid(gate)
    act = (gate * sig * up).astype(bf)
    down_part = dot(act, wd, 1, 0, bf)
    act_grad = dot(dy_all, wd, 1, 1)
    gate_grad = (act_grad * up * sig * (1.0 + gate * (1.0 - sig))).astype(bf)
    up_grad = (act_grad * gate * sig).astype(bf)
    both_grad = jnp.concatenate([gate_grad, up_grad], axis=1)
    wd_grad = dot(act, dy_all, 0, 0, bf).reshape(n_dp, units // n_dp, wide)
    wd_grad = lax.psum_scatter(wd_grad, "dp", scatter_dimension=0)
    wgu_grad = dot(normed2, both_grad, 0, 0, bf)
    wgu_grad = wgu_grad.reshape(2, n_dp, half_wide // n_dp, 2 * units).transpose(1, 0, 2, 3)
    wgu_grad = wgu_grad.reshape(n_dp, wide // n_dp, 2 * units)
    wgu_grad = lax.psum_scatter(wgu_grad, "dp", scatter_dimension=0)
    wgu_grad = wgu_grad.reshape(2, half_wide // n_dp, 2 * units)
    n2_grad = reduce_all(dot(both_grad, wgu, 1, 1, bf))
    block_own = (hidden + reduce_all(down_part)).astype(bf)
    block_output = spread(block_own, rows_all)

    wd_sent = swap(half_of(wd_grad, 1 - row, 1))
    wd_pair = in_order(row, half_of(wd_grad, row, 1)[None], wd_sent[None], 0)
    wd_full = lax.all_gather(wd_pair, "dp", axis=0)
    w_down_grad = wd_full.transpose(1, 0, 2, 3).reshape(2 * units, half_wide).astype(f32)
    wgu_sent = swap(lax.dynamic_index_in_dim(wgu_grad, 1 - row, 0))
    wgu_pair = in_order(row, lax.dynamic_index_in_dim(wgu_grad, row, 0), wgu_sent, 0)
    wgu_full = lax.all_gather(wgu_pair, "dp", axis=0)
    wgu_full = wgu_full.reshape(n_dp, 2, half_wide // n_dp, 2, units).transpose(3, 0, 2, 1, 4)
    wgu_full = wgu_full.reshape(2, half_wide, 2 * units).astype(f32)
    w_gate_grad, w_up_grad = wgu_full[0], wgu_full[1]

    ffn_gain_grad = jnp.sum(n2_grad * hidden * inv2, axis=0)
    scaled2 = n2_grad * g2
    hidden_grad = lax.dynamic_slice_in_dim(
        dy_all, (row * 4 + col) * rows_own, rows_own, 0
    ).astype(f32) + inv2 * (
        scaled2
        - hidden * inv2 * inv2 * jnp.sum(scaled2 * hidden, axis=1, keepdims=True) / wide
    )
    hidden_b = gather_col(hidden_grad.astype(bf))

    wo_grad = dot(attn_rows, hidden_b, 0, 0, bf)
    wo_grad = half_of(wo_grad, row, 1) + swap(half_of(wo_grad, 1 - row, 1))
    w_out_grad = lax.psum(wo_grad, "dp").astype(f32)
    mixed_grad = dot(hidden_b, wo, 1, 1, bf).reshape(seqs, SEQ_LEN, kv_local, GROUP, HD)
    probs = jnp.exp(scores - lse)
    value_grad = jnp.einsum("skpij,sikph->sjkh", probs_b, mixed_grad, preferred_element_type=f32)
    prob_grad = jnp.einsum("sikph,sjkh->skpij", mixed_grad, vals, preferred_element_type=f32)
    delta = jnp.sum(mixed_grad.astype(f32) * mixed.astype(f32), axis=-1)
    delta = jnp.transpose(delta, (0, 2, 3, 1))[..., None]
    score_grad = (probs * (prob_grad - delta)).astype(bf)
    query_grad = rotate(
        jnp.einsum("skpij,sjkh->sikph", score_grad, keys, preferred_element_type=f32) * scale,
        cq,
        sq,
        -1.0,
    )
    key_grad = rotate(
        jnp.einsum("skpij,sikph->sjkh", score_grad, queries, preferred_element_type=f32) * scale,
        ck,
        sk,
        -1.0,
    )
    packed = jnp.concatenate(
        [query_grad, key_grad[:, :, :, None], value_grad[:, :, :, None]], axis=3
    ).astype(bf)
    qkv_grad = packed.reshape(rows_half, w_qkv.shape[1])
    wq_grad = dot(normed1, qkv_grad, 0, 0, bf)
    wq_grad = half_of(wq_grad, row, 0) + swap(half_of(wq_grad, 1 - row, 0))
    w_qkv_grad = lax.psum(wq_grad, "dp").astype(f32)
    n1_grad = reduce_col(dot(qkv_grad, wq, 1, 1, bf))

    attn_gain_grad = jnp.sum(n1_grad * x_own * inv1_own, axis=0)
    scaled1 = n1_grad * g1
    input_own = (
        hidden_grad
        + inv1_own
        * (
            scaled1
            - x_own * inv1_own * inv1_own * jnp.sum(scaled1 * x_own, axis=1, keepdims=True) / wide
        )
    ).astype(bf)
    input_grad = spread(input_own, rows_all)
    gain_grads = lax.psum(jnp.stack([attn_gain_grad, ffn_gain_grad]), ("dp", "row", "col"))
    gain_grads = half_of(gain_grads, row, 1)
    return (
        block_output,
        input_grad,
        gain_grads[0],
        w_qkv_grad,
        w_out_grad,
        gain_grads[1],
        w_gate_grad,
        w_up_grad,
        w_down_grad,
    )


def solution(mesh):
    assert mesh.shape["row"] == 2 and mesh.shape["col"] == 4
    return jax.shard_map(
        body,
        mesh=mesh,
        in_specs=(
            P("dp", "row"),
            P("dp"),
            P("row"),
            P("row", "col"),
            P("col", "row"),
            P("row"),
            P("row", "col"),
            P("row", "col"),
            P("col", "row"),
            P("dp", "row"),
        ),
        out_specs=(
            P("dp", "row"),
            P("dp", "row"),
            P("row"),
            P("row", "col"),
            P("col", "row"),
            P("row"),
            P("row", "col"),
            P("row", "col"),
            P("col", "row"),
        ),
        check_vma=False,
    )
```

time: 1490 us -> 662 us (0.44)
  waiting for transfers between devices: 1230 us -> 77.1 us
  Pallas kernels: 0 us -> 308 us
  local copies, waits for them, and re-layouts: 33.1 us -> 64.9 us
  other arithmetic: 66.5 us -> 37.3 us
  matrix products: 112 us -> 96.5 us
    psum x4 -> x1, waiting for transfers between devices: 622 us -> 0.01 us  [body(): w_qkv_grad = lax.psum(wq_grad, 'dp').astype(f32)]
    reduce_scatter x5 -> x2, waiting for transfers between devices: 394 us -> 0.04 us  [the longest x1 0.02 us: body(): wd_grad = lax.psum_scatter(wd_grad, 'dp', scatter_dimension=0)]
    pallas_call x0 -> x9, Pallas kernels: none -> 308 us  [comm_call(): pl.pallas_call(kernel, out_shape=outs, in_specs=[pl.BlockSpec(memory_spac...]
    all_gather x5 -> x2, waiting for transfers between devices: 211 us -> 23.5 us  [the longest x1 23.5 us: body(): wgu_full = lax.all_gather(wgu_pair, 'dp', axis=0)]
    ppermute x0 -> x9, waiting for transfers between devices: none -> 53.5 us  [swap(): return lax.ppermute(values, 'row', [(0, 1), (1, 0)])]
    convert_element_type x12 -> x6, other arithmetic: 35.8 us -> 13.9 us  [the longest x1 3.97 us: body(): hidden_b = gather_col(hidden_grad.astype(bf))]
    slice x3 -> x7, local copies, waits for them, and re-layouts: 1.48 us -> 21.2 us  [the longest x3 19.2 us: body(): w_gate_grad, w_up_grad = (wgu_full[0], wgu_full[1])]
    dot_general x15 -> x12, matrix products: 97.3 us -> 79.3 us  [dot(): lax.dot_general(left, right, (((lhs,), (rhs,)), ((), ())), preferred_elem...]
  transfers between devices with their start and end apart: 14 -> 14, of which waited for: 14 -> 5; matrix products, arithmetic and copies ran while one was open for 7% -> 19% of each run, Pallas kernels for 0% -> 47%
where the time goes in v1:
time: 662 us; the launch traced here: 652 us
  Pallas kernels  308 us (47%)
  matrix products  96.5 us (15%)
  waiting for transfers between devices  77.1 us (12%)
  local copies, waits for them, and re-layouts  64.9 us (10%)
  blocking collectives  42.7 us (6%)
  other arithmetic  37.3 us (6%)
  between operations  15 us (2%)
  starting transfers between devices  10.5 us (2%)
    pallas_call x9, Pallas kernels, comm_call(): pl.pallas_call(kernel, out_shape=outs, in_specs=[pl.BlockSpec(memory_spac...  308 us
    dot_general x12, matrix products, dot(): lax.dot_general(left, right, (((lhs,), (rhs,)), ((), ())), preferred_elem...  79.3 us
    ppermute x9, waiting for transfers between devices, swap(): return lax.ppermute(values, 'row', [(0, 1), (1, 0)])  53.5 us
    psum x1, blocking collectives, body(): lax.psum(jnp.stack([attn_gain_grad, ffn_gain_grad]), ('dp', 'row', 'col'))  42.7 us
    all_gather x1, waiting for transfers between devices, body(): wgu_full = lax.all_gather(wgu_pair, 'dp', axis=0)  23.5 us
    slice x3, local copies, waits for them, and re-layouts, body(): w_gate_grad, w_up_grad = (wgu_full[0], wgu_full[1])  19.2 us
    unnamed x115, local copies, waits for them, and re-layouts  14.5 us
  transfers between devices with their start and end apart: 14, of which 5 were waited for; matrix products, arithmetic and copies ran while one was open for 19% of the time, Pallas kernels for 47%

profile of v1, /device:TPU:0, one launch (start us, length us, event | category | flops | bytes accessed | tf_op | source)
XLA Modules:
  0.0 651.7 jit_solution(13339251411435906603)
XLA Ops:
  12.9 67.0 %shard_map.169 = (bf16[1024,1536]{1,0:T(8,128)(2,1)}, bf16[2048,1536]{1,0:T(8,128)(2,1)}) custom-call(bf16[2048,768]{1,0:T(8,128)(2,1)} %x_ref.1, bf16[2048,768]{1,0:T(8,128)(2,1)} %dy_ref.1), custom_call_target="tpu_custom_call" | custom-call | bytes 37748736 | tf_op jit(solution)/shard_map/pallas_call | solution.py:63
  86.3 7.0 %fusion.25 = f32[1024,768]{0,1:T(8,128)} fusion(bf16[1024,1536]{1,0:T(8,128)(2,1)S(1)} %copy-done.4, f32[1536]{0:T(1024)S(1)} %get-tuple-element.30, f32[1024]{0:T(1024)} %add_rsqrt_fusion, bf16[768,768]{1,0:T(8,128)(2,1)} %collective-permute-done.1, bf16[768,768]{1,0:T(8,128)(2,1)} %param.13, pred[]{:T(512)S(6)} %eq.2), kind=kOutput, calls=%fused_computation.70 | convolution fusion | flops 2432827392 | bytes 8660993 | tf_op jit(solution)/shard_map/dot_general | solution.py:429
  93.4 4.2 reshape.237
  111.2 5.6 fusion.19
  122.6 5.2 convolution_convert_fusion.4.p_ref
  127.8 23.2 %shard_map.170 = f32[256,1536]{1,0:T(8,128)} custom-call(bf16[1024,1536]{1,0:T(8,128)(2,1)} %convolution_convert_fusion.4.p_ref), custom_call_target="tpu_custom_call" | custom-call | bytes 9437184 | tf_op jit(solution)/shard_map/pallas_call | solution.py:63
  154.0 48.6 %shard_map.171 = bf16[2048,1536]{1,0:T(8,128)(2,1)} custom-call(bf16[256,1536]{1,0:T(8,128)(2,1)} %multiply_convert_fusion.3.h_ref), custom_call_target="tpu_custom_call" | custom-call | bytes 15728640 | tf_op jit(solution)/shard_map/pallas_call | solution.py:63
  202.6 10.6 %fusion.27 = f32[2048,1024]{0,1:T(8,128)S(1)} fusion(bf16[2048,1536]{1,0:T(8,128)(2,1)} %shard_map.171, bf16[768,1024]{0,1:T(8,128)(2,1)} %collective-permute-done.3, bf16[768,1024]{0,1:T(8,128)(2,1)S(1)} %bitcast.139, pred[]{:T(512)S(6)} %eq.2), kind=kOutput, calls=%fused_computation.80 | convolution fusion | flops 6456606720 | bytes 17825792 | tf_op jit(solution)/shard_map/dot_general | solution.py:429
  213.2 9.3 %multiply_convert_fusion.1 = (bf16[2048,512]{0,1:T(8,128)(2,1)}, bf16[2048,512]{0,1:T(8,128)(2,1)}, bf16[2048,512]{0,1:T(8,128)(2,1)S(1)}) fusion(f32[2048,1024]{0,1:T(8,128)S(1)} %fusion.27, bf16[2048,1536]{1,0:T(8,128)(2,1)} %get-tuple-element.22, bf16[512,768]{1,0:T(8,128)(2,1)S(1)} %collective-permute-done.4, ...), kind=kOutput, calls=%fused_computation.17 | convolution fusion | flops 3245080576 | bytes 22544384 | tf_op jit(solution)/shard_map/dot_general | solution.py:429
  222.6 4.5 convolution_convert_fusion.6
  227.2 12.4 %convolution_convert_fusion.p_ref = bf16[2048,1536]{1,0:T(8,128)(2,1)} fusion(bf16[2048,512]{0,1:T(8,128)(2,1)} %get-tuple-element.38, bf16[2048,512]{0,1:T(8,128)(2,1)} %get-tuple-element.37, bf16[768,1024]{0,1:T(8,128)(2,1)} %collective-permute-done.3, bf16[768,1024]{0,1:T(8,128)(2,1)S(1)} %bitcast.140, pred[]{:T(512)S(6)} %eq.2), kind=kOutput, calls=%fused_computation.8 | convolution fusion | flops 6468141056 | bytes 13631489 | tf_op jit(solution)/shard_map/dot_general | solution.py:429
  239.6 35.4 %shard_map.174 = f32[256,1536]{1,0:T(8,128)} custom-call(bf16[2048,1536]{1,0:T(8,128)(2,1)} %convolution_convert_fusion.p_ref), custom_call_target="tpu_custom_call" | custom-call | bytes 18874368 | tf_op jit(solution)/shard_map/pallas_call | solution.py:63
  275.0 5.8 convolution_convert_fusion.1.p_ref
  280.8 34.8 %shard_map.172 = f32[256,1536]{1,0:T(8,128)} custom-call(bf16[2048,1536]{1,0:T(8,128)(2,1)} %convolution_convert_fusion.1.p_ref), custom_call_target="tpu_custom_call" | custom-call | bytes 18874368 | tf_op jit(solution)/shard_map/pallas_call | solution.py:63
  315.6 8.8 %convolution_convert_fusion.2 = bf16[1536,1024]{1,0:T(8,128)(2,1)S(1)} fusion(bf16[2048,1536]{1,0:T(8,128)(2,1)} %shard_map.171, bf16[2048,512]{0,1:T(8,128)(2,1)S(1)} %copy-done.49, bf16[2048,512]{0,1:T(8,128)(2,1)S(1)} %copy-done.48), kind=kOutput, calls=%fused_computation.20 | convolution fusion | flops 6452412416 | bytes 13631488 | tf_op jit(solution)/shard_map/dot_general | solution.py:429
  327.7 4.0 fusion.48
  331.7 24.3 %shard_map.175 = bf16[1024,1536]{1,0:T(8,128)(2,1)} custom-call(bf16[256,1536]{1,0:T(8,128)(2,1)} %get-tuple-element.33.h_ref), custom_call_target="tpu_custom_call" | custom-call | bytes 9437184 | tf_op jit(solution)/shard_map/pallas_call | solution.py:63
  356.0 4.4 convolution_convert_fusion.8
  362.8 5.3 fusion.1
  376.8 3.8 convolution_convert_fusion.5
  386.5 36.6 %collective-permute-done.6 = bf16[384,768]{1,0:T(8,128)(2,1)} collective-permute-done((bf16[384,768]{1,0:T(8,128)(2,1)}, bf16[384,768]{1,0:T(8,128)(2,1)}, u32[]{:S(2)}, u32[]{:S(2)}) %collective-permute-start.6) | collective-permute-done | bytes 589856 | tf_op jit(solution)/shard_map/ppermute | solution.py:435
  430.6 5.2 collective-permute-done.8
  439.1 8.6 %collective-permute-done.7 = bf16[1,192,1024]{2,1,0:T(8,128)(2,1)S(1)} collective-permute-done((bf16[1,192,1024]{2,1,0:T(8,128)(2,1)S(1)}, bf16[1,192,1024]{2,1,0:T(8,128)(2,1)S(1)}, u32[]{:S(2)}, u32[]{:S(2)}) %collective-permute-start.7) | collective-permute-done | bytes 393248 | tf_op jit(solution)/shard_map/ppermute | solution.py:435
  448.7 24.3 %shard_map.173 = bf16[2048,768]{1,0:T(8,128)(2,1)} custom-call(bf16[256,1536]{1,0:T(8,128)(2,1)} %get-tuple-element.50.h_ref), custom_call_target="tpu_custom_call" | custom-call | bytes 25165824 | tf_op jit(solution)/shard_map/pallas_call | solution.py:63
  473.0 6.0 convolution_convert_fusion.3.p_ref
  479.1 25.0 %shard_map.176 = f32[256,1536]{1,0:T(8,128)} custom-call(bf16[1024,1536]{1,0:T(8,128)(2,1)} %convolution_convert_fusion.3.p_ref), custom_call_target="tpu_custom_call" | custom-call | bytes 9437184 | tf_op jit(solution)/shard_map/pallas_call | solution.py:63
  507.5 25.3 %shard_map.177 = bf16[2048,768]{1,0:T(8,128)(2,1)} custom-call(bf16[256,1536]{1,0:T(8,128)(2,1)} %fusion.13.h_ref), custom_call_target="tpu_custom_call" | custom-call | bytes 25165824 | tf_op jit(solution)/shard_map/pallas_call | solution.py:63
  532.8 42.7 %psum.21 = f32[2,1536]{1,0:T(2,128)S(1)} all-reduce(f32[2,1536]{1,0:T(2,128)S(1)} %pad_maximum_fusion.7), channel_id=1, replica_groups=mesh['dp'=4,'row'=2,'col'=4] {'dp','row','col'}, use_global_device_ids=true, to_apply=%region_9.10 | all-reduce | flops 3072 | bytes 24576 | tf_op jit(solution)/shard_map/psum | solution.py:592
  583.6 23.5 %all-gather.3.cloned.1.call-done = bf16[4,2,192,1024]{3,2,1,0:T(8,128)(2,1)} async-done(((bf16[1,2,192,1024]{3,2,1,0:T(8,128)(2,1)}), bf16[4,2,192,1024]{3,2,1,0:T(8,128)(2,1)}) %all-gather.3.cloned.1.call-update) | async-done | bytes 3145744 | tf_op jit(solution)/shard_map/all_gather | solution.py:535
  607.1 9.2 %reshape.246 = f32[4,2,192,2,512]{4,3,2,1,0:T(2,128)} reshape(bf16[4,2,192,1024]{3,2,1,0:T(8,128)(2,1)} %all-gather.3.cloned.1.call-done) | data formatting | bytes 9437184 | tf_op jit(solution)/shard_map/convert_element_type | solution.py:537
  616.3 12.4 %fusion.49 = (f32[1,4,192,2,512]{4,0,2,3,1:T(1,128)S(1)}, f32[1,4,192,2,512]{4,0,2,3,1:T(1,128)}) fusion(f32[2,4,192,2,512]{4,0,2,3,1:T(2,128)} %bitcast.121), kind=kLoop, calls=%fused_computation.128 | loop fusion | bytes 12582912 | tf_op jit(solution)/shard_map/slice | solution.py:538
  628.7 4.3 copy.83
  (207 shorter events, 89.4 us)
Async XLA Ops:
  7.2 421.1 %reduce-scatter.5.cloned.1.call-start = ((), (), s32[]{:S(2)}) async-start(), calls=%async_computation.4 | async-start | bytes 1966080 | tf_op jit(solution)/shard_map/reduce_scatter | solution.py:519
  9.2 76.3 %collective-permute-start = (f32[2,768]{1,0:T(2,128)}, f32[2,768]{1,0:T(2,128)}, u32[]{:S(2)}, u32[]{:S(2)}) collective-permute-start(f32[2,768]{1,0:T(2,128)} %pad_maximum_fusion.8), channel_id=1, source_target_pairs={{0,4},{4,0},{1,5},{5,1},{2,6},{6,2},{3,7},{7,3},{8,12},{12,8},{9,1... | collective-permute-start | bytes 18440 | tf_op jit(solution)/shard_map/ppermute | solution.py:435
  12.2 74.1 %collective-permute-start.1 = (bf16[768,768]{1,0:T(8,128)(2,1)}, bf16[768,768]{1,0:T(8,128)(2,1)}, u32[]{:S(2)}, u32[]{:S(2)}) collective-permute-start(bf16[768,768]{1,0:T(8,128)(2,1)} %param.13), channel_id=1, source_target_pairs={{0,4},{4,0},{1,5},{5,1},{2,6},{6,2},{3,7},{7,3},{8,12},{12,8},{9,1... | collective-permute-start | bytes 3538952 | tf_op jit(solution)/shard_map/ppermute | solution.py:435
  79.9 6.4 copy-start.4
  106.1 16.5 %collective-permute-start.2 = (bf16[384,768]{1,0:T(8,128)(2,1)}, bf16[384,768]{1,0:T(8,128)(2,1)}, u32[]{:S(2)}, u32[]{:S(2)}) collective-permute-start(bf16[384,768]{1,0:T(8,128)(2,1)} %param.14), channel_id=1, source_target_pairs={{0,4},{4,0},{1,5},{5,1},{2,6},{6,2},{3,7},{7,3},{8,12},{12,8},{9,1... | collective-permute-start | bytes 1769480 | tf_op jit(solution)/shard_map/ppermute | solution.py:435
  109.8 92.8 %copy-start.21 = (bf16[768,2,512]{0,2,1:T(8,128)(2,1)}, bf16[768,2,512]{0,2,1:T(8,128)(2,1)S(1)}, u32[]{:S(2)}) copy-start(bf16[768,2,512]{0,2,1:T(8,128)(2,1)S(1)} %get-tuple-element.42) | copy-start | bytes 4718596
  109.8 92.8 %collective-permute-start.3 = (bf16[768,1024]{0,1:T(8,128)(2,1)S(1)}, bf16[768,1024]{0,1:T(8,128)(2,1)}, u32[]{:S(2)}, u32[]{:S(2)}) collective-permute-start(bf16[768,1024]{0,1:T(8,128)(2,1)S(1)} %bitcast.141), channel_id=1, source_target_pairs={{0,4},{4,0},{1,5},{5,1},{2,6},{6,2},{3,7},{7,3},{8,12},{12,8},{9,1... | collective-permute-start | bytes 4718600 | tf_op jit(solution)/shard_map/ppermute | solution.py:435
  118.7 94.6 %copy-start.33 = (bf16[512,768]{1,0:T(8,128)(2,1)}, bf16[512,768]{1,0:T(8,128)(2,1)S(1)}, u32[]{:S(2)}) copy-start(bf16[512,768]{1,0:T(8,128)(2,1)S(1)} %get-tuple-element.51) | copy-start | bytes 2359300
  118.7 94.5 %collective-permute-start.4 = (bf16[512,768]{1,0:T(8,128)(2,1)S(1)}, bf16[512,768]{1,0:T(8,128)(2,1)S(1)}, u32[]{:S(2)}, u32[]{:S(2)}) collective-permute-start(bf16[512,768]{1,0:T(8,128)(2,1)S(1)} %get-tuple-element.52), channel_id=1, source_target_pairs={{0,4},{4,0},{1,5},{5,1},{2,6},{6,2},{3,7},{7,3},{8,12},{12,8},{9,1... | collective-permute-start | bytes 2359304 | tf_op jit(solution)/shard_map/ppermute | solution.py:435
  152.9 49.7 %copy-start.38 = (f32[256]{0:T(256)}, f32[256]{0:T(256)S(1)}, u32[]{:S(2)}) copy-start(f32[256]{0:T(256)S(1)} %add_rsqrt_fusion.1) | copy-start | bytes 3076
  202.6 19.9 %slice-start.2 = ((s8[6291456]{0:T(1024)(128)(4,1)}), s8[4194304]{0:T(1024)(128)(4,1)S(1)}, s32[]{:S(2)}) async-start(s8[6291456]{0:T(1024)(128)(4,1)} %bitcast.147), calls=%async_computation.9 | async-start | bytes 8388608
  213.2 9.3 %copy-start.44 = (bf16[512,768]{1,0:T(8,128)(2,1)}, bf16[512,768]{1,0:T(8,128)(2,1)S(1)}, u32[]{:S(2)}) copy-start(bf16[512,768]{1,0:T(8,128)(2,1)S(1)} %collective-permute-done.4) | copy-start | bytes 2359300
  213.2 9.3 %slice-start.3 = ((s8[6291456]{0:T(1024)(128)(4,1)}), s8[2097152]{0:T(1024)(128)(4,1)S(1)}, s32[]{:S(2)}) async-start(s8[6291456]{0:T(1024)(128)(4,1)} %bitcast.147), calls=%async_computation.10 | async-start | bytes 4194304
  227.1 209.6 %reduce-scatter.3.cloned.1.call-start = ((), (), s32[]{:S(2)}) async-start(), calls=%async_computation.2 | async-start | bytes 3932160 | tf_op jit(solution)/shard_map/reduce_scatter | solution.py:523
  239.6 35.4 %copy-start.34 = (bf16[512,768]{1,0:T(8,128)(2,1)S(1)}, bf16[512,768]{1,0:T(8,128)(2,1)}, u32[]{:S(2)}) copy-start(bf16[512,768]{1,0:T(8,128)(2,1)} %copy-done.33) | copy-start | bytes 2359300
  239.6 35.4 %copy-start.45 = (bf16[512,768]{1,0:T(8,128)(2,1)S(1)}, bf16[512,768]{1,0:T(8,128)(2,1)}, u32[]{:S(2)}) copy-start(bf16[512,768]{1,0:T(8,128)(2,1)} %copy-done.44) | copy-start | bytes 2359300
  239.6 35.4 %copy-start.47 = (bf16[2048,512]{0,1:T(8,128)(2,1)S(1)}, bf16[2048,512]{0,1:T(8,128)(2,1)}, u32[]{:S(2)}) copy-start(bf16[2048,512]{0,1:T(8,128)(2,1)} %copy-done.46) | copy-start | bytes 6291460
  280.8 34.8 %copy-start.48 = (bf16[2048,512]{0,1:T(8,128)(2,1)S(1)}, bf16[2048,512]{0,1:T(8,128)(2,1)}, u32[]{:S(2)}) copy-start(bf16[2048,512]{0,1:T(8,128)(2,1)} %get-tuple-element.37) | copy-start | bytes 6291460
  280.8 34.8 %copy-start.49 = (bf16[2048,512]{0,1:T(8,128)(2,1)S(1)}, bf16[2048,512]{0,1:T(8,128)(2,1)}, u32[]{:S(2)}) copy-start(bf16[2048,512]{0,1:T(8,128)(2,1)} %get-tuple-element.38) | copy-start | bytes 6291460
  327.7 248.6 %all-reduce.3.cloned.1.call-start = ((), (), s32[]{:S(2)}) async-start(), calls=%async_computation.6 | async-start | bytes 3538944 | tf_op jit(solution)/shard_map/psum | solution.py:578
  376.8 6.2 copy-start.10
  376.8 6.2 copy-start.32
  381.9 43.4 %collective-permute-start.5 = (bf16[768,768]{1,0:T(8,128)(2,1)}, bf16[768,768]{1,0:T(8,128)(2,1)}, u32[]{:S(2)}, u32[]{:S(2)}) collective-permute-start(bf16[768,768]{1,0:T(8,128)(2,1)} %constant_dynamic-slice_fusion.2), channel_id=1, source_target_pairs={{0,4},{4,0},{1,5},{5,1},{2,6},{6,2},{3,7},{7,3},{8,12},{12,8},{9,1... | collective-permute-start | bytes 3538952 | tf_op jit(solution)/shard_map/ppermute | solution.py:435
  385.6 37.5 %collective-permute-start.6 = (bf16[384,768]{1,0:T(8,128)(2,1)}, bf16[384,768]{1,0:T(8,128)(2,1)}, u32[]{:S(2)}, u32[]{:S(2)}) collective-permute-start(bf16[384,768]{1,0:T(8,128)(2,1)} %constant_dynamic-slice_fusion.1), channel_id=1, source_target_pairs={{0,4},{4,0},{1,5},{5,1},{2,6},{6,2},{3,7},{7,3},{8,12},{12,8},{9,1... | collective-permute-start | bytes 1769480 | tf_op jit(solution)/shard_map/ppermute | solution.py:435
  428.2 152.0 %all-gather.5.cloned.1.call-start = ((), (), s32[]{:S(2)}) async-start(), calls=%async_computation.5 | async-start | bytes 1966080 | tf_op jit(solution)/shard_map/all_gather | solution.py:531
  429.4 6.4 collective-permute-start.8
  436.6 170.5 %all-gather.3.cloned.1.call-start = ((), (), s32[]{:S(2)}) async-start(), calls=%async_computation.3 | async-start | bytes 3932160 | tf_op jit(solution)/shard_map/all_gather | solution.py:535
  437.9 9.8 %collective-permute-start.7 = (bf16[1,192,1024]{2,1,0:T(8,128)(2,1)S(1)}, bf16[1,192,1024]{2,1,0:T(8,128)(2,1)S(1)}, u32[]{:S(2)}, u32[]{:S(2)}) collective-permute-start(bf16[1,192,1024]{2,1,0:T(8,128)(2,1)S(1)} %get-tuple-element.58), channel_id=1, source_target_pairs={{0,4},{4,0},{1,5},{5,1},{2,6},{6,2},{3,7},{7,3},{8,12},{12,8},{9,1... | collective-permute-start | bytes 1179656 | tf_op jit(solution)/shard_map/ppermute | solution.py:435
  448.7 24.3 %copy-start.16 = (bf16[96,8,2,512]{3,1,2,0:T(8,128)(2,1)S(1)}, bf16[96,8,2,512]{3,1,2,0:T(8,128)(2,1)}, u32[]{:S(2)}) copy-start(bf16[96,8,2,512]{3,1,2,0:T(8,128)(2,1)} %copy-done.15) | copy-start | bytes 4718596
  448.7 24.3 %copy-start.43 = (bf16[768,768]{1,0:T(8,128)(2,1)S(1)}, bf16[768,768]{1,0:T(8,128)(2,1)}, u32[]{:S(2)}) copy-start(bf16[768,768]{1,0:T(8,128)(2,1)} %param.13) | copy-start | bytes 3538948
  479.1 26.9 %copy-start.7 = (f32[256,1536]{1,0:T(8,128)S(1)}, f32[256,1536]{1,0:T(8,128)}, u32[]{:S(2)}) copy-start(f32[256,1536]{1,0:T(8,128)} %get-tuple-element.34) | copy-start | bytes 4718596
  507.5 25.3 %copy-start.37 = (f32[1536]{0:T(1024)S(1)}, f32[1536]{0:T(1024)}, u32[]{:S(2)}) copy-start(f32[1536]{0:T(1024)} %get-tuple-element.25) | copy-start | bytes 18436
  (36 other events, 93.7 us)
Sparse Core Ops, SparseCore 0:
  227.2 34.9 reduce-scatter.4
  327.8 60.6 reduce-scatter.2
  428.4 75.7 all-reduce.2
  506.1 36.0 all-gather.4
  544.2 62.8 all-gather.2
